TPU v7x, 32 devices: a whole 2x2x4 slice. The times are simulated.
32 devices in a mesh: row: 4 (over z), col: 8 (over y, x, core).
Axes of the slice: x: 2, y: 2, z: 4, core: 2. Of those that a mesh axis runs over, the one named last changes fastest.
Arguments:
- a_matrix: bfloat16 [8192, 8192], P('row', 'col'), may hold values from -6 to 6
- a_flags: int32 [64, 64], P('row', 'col'), may hold values from 0 to 1, as said below
- b_matrix: bfloat16 [8192, 16384], P('row', 'col'), may hold values from -0.1875 to 0.1875
- b_flags: int32 [64, 128], P('row', 'col'), may hold values from 0 to 1, as said below
- sections: int32 [2], replicated, may hold values from 0 to 7
Outputs:
- packed: bfloat16 [8192, 16384], P('row', 'col')
- tile_place: int32 [64, 128], P('row', 'col')
Inputs may be any that keep to these rules, and one draw needn't show every extreme that they name: `a_flags`: 0 or 1; the 16 x 8 tiles of one device hold at most 64 ones, and some device holds exactly 64. `b_flags`: 0 or 1; each aligned block of 8 x 16 tiles holds at most 64 ones, and some block exactly 64.
All inputs are finite; a program needn't handle non-finite values.
Results may differ from a plain program's by a relative error of at most 0.001.
Values may be sent and summed in bfloat16 or wider, within the bound.
A program may use at most 128 MiB of HBM per device.

v0:
```python
import jax
import jax.numpy as jnp
from jax import lax
from jax.sharding import PartitionSpec as P

TILE = 128
SECTIONS = 2
MOST = 64


def spread(value, axis, source):
    kept = jnp.where(lax.axis_index(axis) == source, value, 0).astype(value.dtype)
    return lax.psum(kept, axis)


def prefix(value, axis, combine, identity):
    length, position = (lax.axis_size(axis), lax.axis_index(axis))
    everything = lax.all_gather(value, axis)
    start = jnp.broadcast_to(jnp.asarray(identity, value.dtype), value.shape)

    def lap(k, before):
        reached = k < position
        new = combine(before, everything[k])
        return jnp.where(reached, new, before)

    return lax.fori_loop(0, length, lap, start)


def to_tiles(matrix, tile_rows, tile_cols):
    return (
        matrix.reshape(tile_rows, TILE, tile_cols, TILE)
        .transpose(0, 2, 1, 3)
        .reshape(tile_rows * tile_cols, TILE, TILE)
    )


def from_tiles(tiles, tile_rows, tile_cols):
    return (
        tiles.reshape(tile_rows, tile_cols, TILE, TILE)
        .transpose(0, 2, 1, 3)
        .reshape(tile_rows * TILE, tile_cols * TILE)
    )


def mask_tiles(matrix, flags, tile_rows, tile_cols):
    shaped = matrix.reshape(tile_rows, TILE, tile_cols, TILE)
    shaped = shaped * flags[:, None, :, None]
    return shaped.reshape(tile_rows * TILE, tile_cols * TILE)


def compact(tiles, flags_flat, capacity):
    rank_of = jnp.cumsum(flags_flat) - 1
    slot_ids = jnp.arange(capacity, dtype=jnp.int32)
    matched = (flags_flat[None, :] == 1) & (rank_of[None, :] == slot_ids[:, None])
    source = jnp.sum(
        jnp.where(matched, jnp.arange(flags_flat.shape[0], dtype=jnp.int32)[None, :], 0), axis=1
    )
    is_valid = jnp.any(matched, axis=1)
    return jnp.take(tiles, source, axis=0) * is_valid.astype(tiles.dtype)[:, None, None]


def expand(packed_tiles, flags_flat, capacity):
    rank_of = jnp.cumsum(flags_flat) - 1
    position = jnp.where(flags_flat == 1, rank_of, capacity)
    extended = jnp.concatenate(
        [packed_tiles, jnp.zeros((1, TILE, TILE), packed_tiles.dtype)], axis=0
    )
    return jnp.take(extended, position, axis=0)


def add_up(earlier, later):
    return earlier + later


def shards(a_matrix, a_flags, b_matrix, b_flags, sections):
    tile_rows, panel_cols = a_flags.shape
    tile_cols = b_flags.shape[1]
    row_ratio = lax.axis_size("col") // lax.axis_size("row")
    panel_width = panel_cols * TILE
    a_send_flags = a_flags.astype(jnp.bfloat16)
    product = jnp.zeros((tile_rows * TILE, tile_cols * TILE), jnp.float32)
    intersection = jnp.zeros((tile_rows, tile_cols), jnp.float32)
    for step_index in range(SECTIONS):
        section = sections[step_index]
        owner_row = section // row_ratio
        start_tile = section % row_ratio * panel_cols
        b_panel = lax.dynamic_slice_in_dim(b_matrix, start_tile * TILE, panel_width, 0)
        b_panel_flags = lax.dynamic_slice_in_dim(b_flags, start_tile, panel_cols, 0)
        b_send_flags = b_panel_flags.astype(jnp.bfloat16)
        a_packed = compact(to_tiles(a_matrix, tile_rows, panel_cols), a_flags.reshape(-1), MOST)
        b_packed = compact(
            to_tiles(b_panel, panel_cols, tile_cols), b_panel_flags.reshape(-1), MOST
        )
        a_recv, a_got_flags = (
            spread(a_packed, "col", section),
            spread(a_send_flags, "col", section),
        )
        b_recv, b_got_flags = (
            spread(b_packed, "row", owner_row),
            spread(b_send_flags, "row", owner_row),
        )
        a_got = from_tiles(
            expand(a_recv, a_got_flags.astype(jnp.int32).reshape(-1), MOST), tile_rows, panel_cols
        )
        b_got = from_tiles(
            expand(b_recv, b_got_flags.astype(jnp.int32).reshape(-1), MOST), panel_cols, tile_cols
        )
        a_masked = mask_tiles(a_got, a_got_flags, tile_rows, panel_cols)
        b_masked = mask_tiles(b_got, b_got_flags, panel_cols, tile_cols)
        product = product + jnp.dot(a_masked, b_masked, preferred_element_type=jnp.float32)
        intersection = intersection + jnp.dot(
            a_got_flags.astype(jnp.float32),
            b_got_flags.astype(jnp.float32),
            precision=lax.Precision.HIGHEST,
        )
    occupied = (intersection > 0.5).astype(jnp.int32).reshape(-1)
    filled = jnp.sum(occupied).reshape(1)
    zero_count = jnp.zeros((1,), jnp.int32)
    offset = prefix(filled, ("row", "col"), add_up, zero_count)
    tiles = to_tiles(product.astype(jnp.bfloat16), tile_rows, tile_cols)
    packed = from_tiles(compact(tiles, occupied, tile_rows * tile_cols), tile_rows, tile_cols)
    slot_ids = jnp.arange(tile_rows * tile_cols, dtype=jnp.int32)
    places = jnp.where(slot_ids < filled[0], offset[0] + slot_ids, -1).astype(jnp.int32)
    return (packed, places.reshape(tile_rows, tile_cols))


def solution(mesh):
    return jax.shard_map(
        shards,
        mesh=mesh,
        in_specs=(P("row", "col"), P("row", "col"), P("row", "col"), P("row", "col"), P()),
        out_specs=(P("row", "col"), P("row", "col")),
        check_vma=False,
    )
```

profile of v0, /device:TPU:0, one launch (start us, length us, event | category | flops | bytes accessed | tf_op | source)
XLA Modules:
  0.0 386.4 jit_solution(5069654762923967390)
XLA Ops:
  12.2 3.3 copy.90
  15.8 3.3 copy.72
  30.5 9.1 %dynamic-slice_bitcast_fusion = (bf16[128,8,16,128]{3,1,2,0:T(8,128)(2,1)S(1)}, bf16[128,8,16,128]{3,1,2,0:T(8,128)(2,1)}) fusion(bf16[2048,2048]{1,0:T(8,128)(2,1)} %param.13, s32[]{:T(128)S(6)} %select_n.201, s32[]{:T(128)S(6)} %select_n.193), kind=kLoop, calls=%fused_computation.29 | loop fusion | bytes 16777224
  45.6 3.7 copy.92
  50.0 3.2 copy.77
  56.9 4.7 %gather_fusion.3 = bf16[64,128,128]{2,1,0:T(8,128)(2,1)} fusion(bf16[128,128,128]{2,1,0:T(8,128)(2,1)} %bitcast.100, s32[1024]{0:T(1024)S(1)} %pad_clamp_fusion.5), kind=kCustom, calls=%fused_computation.2.clone | custom fusion | bytes 4194560 | tf_op jit(solution)/shard_map/jit(_take)/gather | solution.py:59
  65.6 13.2 %all-reduce.7 = (bf16[8,16]{1,0:T(8,128)(2,1)S(1)}, bf16[8,16]{1,0:T(8,128)(2,1)S(1)}) all-reduce(bf16[8,16]{1,0:T(8,128)(2,1)S(1)} %get-tuple-element.116, bf16[8,16]{1,0:T(8,128)(2,1)S(1)} %get-tuple-element.108), channel_id=1, replica_groups=mesh['row'=4,'col'=8] {'row'}, use_global_device_ids=true, to_apply=%region_1.2 | all-reduce | flops 256 | bytes 1024 | tf_op jit(solution)/shard_map/psum | solution.py:13
  78.8 11.8 %all-reduce.5 = (bf16[16,8]{0,1:T(8,128)(2,1)S(1)}, bf16[16,8]{0,1:T(8,128)(2,1)S(1)}) all-reduce(bf16[16,8]{0,1:T(8,128)(2,1)S(1)} %get-tuple-element.119, bf16[16,8]{0,1:T(8,128)(2,1)S(1)} %get-tuple-element.118), channel_id=1, replica_groups=mesh['row'=4,'col'=8] {'col'}, use_global_device_ids=true, to_apply=%region_0.1 | all-reduce | flops 256 | bytes 1024 | tf_op jit(solution)/shard_map/psum | solution.py:13
  95.1 40.6 %all-reduce.4 = s32[32]{0:T(128)S(1)} all-reduce(s32[32]{0:T(128)S(1)} %dynamic-update-slice), channel_id=1, replica_groups=mesh['row'=4,'col'=8] {'row','col'}, use_global_device_ids=true, to_apply=%add.4 | all-reduce | flops 32 | bytes 256
  136.2 44.6 %while.13 = (s32[]{:T(128)}, s32[1]{0:T(128)}, s32[]{:T(128)}, s32[32,1]{0,1:T(1,128)S(1)}, s32[]{:T(128)}) while((s32[]{:T(128)}, s32[1]{0:T(128)}, s32[]{:T(128)}, s32[32,1]{0,1:T(1,128)S(1)}, s32[]{:T(128)}) %tuple.62), condition=%wide.region_27.30_spmd, body=%wide.region_26.29_spmd.sunk | while | flops 5 | bytes 107 | solution.py:26
  189.5 4.6 %gather_fusion.5 = bf16[128,128,128]{2,1,0:T(8,128)(2,1)} fusion(bf16[65,128,128]{2,1,0:T(8,128)(2,1)} %concatenate.14, s32[1024]{0:T(1024)S(1)} %pad_clamp_fusion.3), kind=kCustom, calls=%fused_computation.5.clone | custom fusion | bytes 8389120 | tf_op jit(solution)/shard_map/jit(_take)/gather | solution.py:68
  198.8 4.4 %copy_multiply_fusion.3 = bf16[16,8,128,128]{3,1,2,0:T(8,128)(2,1)} fusion(bf16[16,8,128,128]{3,2,1,0:T(8,128)(2,1)S(1)} %bitcast.97, bf16[16,8]{1,0:T(8,128)(2,1)S(1)} %copy.73), kind=kLoop, calls=%fused_computation.28 | loop fusion | flops 2097152 | bytes 8388864 | tf_op jit(solution)/shard_map/mul | solution.py:47
  203.2 4.4 %copy_multiply_fusion.1 = bf16[16,8,128,128]{3,1,2,0:T(8,128)(2,1)} fusion(bf16[16,8,128,128]{3,2,1,0:T(8,128)(2,1)S(1)} %bitcast.98, bf16[16,8]{1,0:T(8,128)(2,1)S(1)} %copy.82), kind=kLoop, calls=%fused_computation.26 | loop fusion | flops 2097152 | bytes 8388864 | tf_op jit(solution)/shard_map/mul | solution.py:47
  207.5 59.3 %all-reduce.14.cloned.1.call-done = (bf16[64,128,128]{2,1,0:T(8,128)(2,1)}, bf16[64,128,128]{2,1,0:T(8,128)(2,1)}) async-done(((bf16[64,128,128]{2,1,0:T(8,128)(2,1)}, bf16[64,128,128]{2,1,0:T(8,128)(2,1)}), (bf16[64,128,128]{2,1,0:T(8,128)(2,1)}, bf16[64,128,128]{2,1,0:T(8,128)(2,1)})) %all-reduce.14.cloned.1.call-update) | async-done | bytes 4194320 | tf_op jit(solution)/shard_map/psum | solution.py:13
  274.4 4.3 %copy_multiply_fusion.2 = bf16[8,16,128,128]{3,1,2,0:T(8,128)(2,1)} fusion(bf16[8,16,128,128]{3,2,1,0:T(8,128)(2,1)S(1)} %bitcast.92, bf16[8,16]{1,0:T(8,128)(2,1)S(1)} %get-tuple-element.96), kind=kLoop, calls=%fused_computation.27 | loop fusion | flops 2097152 | bytes 8388864 | tf_op jit(solution)/shard_map/mul | solution.py:47
  278.9 3.2 gather_fusion.7
  288.2 11.7 %fusion.5 = f32[2048,2048]{1,0:T(8,128)} fusion(bf16[128,8,16,128]{3,2,1,0:T(8,128)(2,1)S(1)} %bitcast.103, bf16[256,8,8,128]{3,2,1,0:T(8,128)(2,1)S(1)} %bitcast.106), kind=kOutput, calls=%fused_computation.18 | convolution fusion | flops 8589934592 | bytes 25165824 | tf_op jit(solution)/shard_map/dot_general | solution.py:110
  299.9 16.3 %fusion = bf16[256,8,16,128]{3,1,2,0:T(8,128)(2,1)} fusion(f32[2048,2048]{1,0:T(8,128)} %fusion.5, bf16[128,8,16,128]{3,2,1,0:T(8,128)(2,1)S(1)} %bitcast.104, bf16[256,8,8,128]{3,2,1,0:T(8,128)(2,1)} %bitcast.107), kind=kOutput, calls=%fused_computation.10 | convolution fusion | flops 8598323200 | bytes 33554432 | tf_op jit(solution)/shard_map/dot_general | solution.py:110
  316.1 9.8 %copy.97 = bf16[256,8,16,128]{3,2,1,0:T(8,128)(2,1)} copy(bf16[256,8,16,128]{3,1,2,0:T(8,128)(2,1)} %fusion) | data formatting | bytes 16777216
  325.9 9.3 %copy.88 = bf16[16,128,16,128]{3,1,2,0:T(8,128)(2,1)} copy(bf16[16,128,16,128]{3,2,1,0:T(8,128)(2,1)} %bitcast.90) | data formatting | bytes 16777216 | tf_op jit(solution)/shard_map/reshape | solution.py:31
  335.2 11.9 %gather_fusion = bf16[256,128,128]{2,1,0:T(8,128)(2,1)} fusion(bf16[256,128,128]{2,1,0:T(8,128)(2,1)} %bitcast.89, s32[1024]{0:T(1024)S(1)} %pad_clamp_fusion), kind=kCustom, calls=%fused_computation.7 | custom fusion | bytes 16778240 | tf_op jit(solution)/shard_map/jit(_take)/gather | solution.py:59
  347.1 7.5 %multiply_bitcast_fusion = bf16[16,128,16,128]{3,1,2,0:T(8,128)(2,1)} fusion(bf16[16,16,128,128]{3,2,1,0:T(8,128)(2,1)} %bitcast.88, pred[16,16]{1,0:T(8,128)(4,1)S(1)} %compare_and_fusion, bf16[16,16]{1,0:T(8,128)(2,1)S(1)} %reshape.414), kind=kLoop, calls=%fused_computation.12 | loop fusion | flops 8388608 | bytes 16777984 | tf_op jit(solution)/shard_map/transpose | solution.py:40
  354.6 13.7 %copy.89 = bf16[16,128,16,128]{3,2,1,0:T(8,128)(2,1)} copy(bf16[16,128,16,128]{3,1,2,0:T(8,128)(2,1)} %multiply_bitcast_fusion) | data formatting | bytes 16777216 | tf_op jit(solution)/shard_map/transpose | solution.py:40
  368.3 11.1 %copy.120 = bf16[256,8,16,128]{3,1,2,0:T(8,128)(2,1)} copy(bf16[256,8,16,128]{3,2,1,0:T(8,128)(2,1)} %bitcast.91) | data formatting | bytes 16777216
  (167 shorter events, 77.4 us)
Async XLA Ops:
  7.2 175.5 %all-reduce.12.cloned.1.call-start = ((), (), s32[]{:S(2)}) async-start(), calls=%async_computation | async-start | bytes 8388608 | tf_op jit(solution)/shard_map/psum | solution.py:13
  22.3 8.0 %copy-start.7 = (s32[16,16]{1,0:T(8,128)S(1)}, s32[16,16]{1,0:T(8,128)}, u32[]{:S(2)}) copy-start(s32[16,16]{1,0:T(8,128)} %param.14) | copy-start | bytes 3076
  24.7 242.2 %all-reduce.14.cloned.1.call-start = ((), (), s32[]{:S(2)}) async-start(), calls=%async_computation.1 | async-start | bytes 8388608 | tf_op jit(solution)/shard_map/psum | solution.py:13
  61.6 2.3 copy-start.1
  63.9 14.9 %copy-start.6 = (s32[16,8]{0,1:T(8,128)S(1)}, s32[16,8]{0,1:T(8,128)}, u32[]{:S(2)}) copy-start(s32[16,8]{0,1:T(8,128)} %param.12) | copy-start | bytes 1540
  182.6 2.3 copy-start.4
  194.1 4.2 %copy-start = (bf16[128,128,128]{2,1,0:T(8,128)(2,1)S(1)}, bf16[128,128,128]{2,1,0:T(8,128)(2,1)}, u32[]{:S(2)}) copy-start(bf16[128,128,128]{2,1,0:T(8,128)(2,1)} %gather_fusion.5) | copy-start | bytes 12582916
  274.4 4.3 %copy-start.5 = (bf16[64,128,128]{2,1,0:T(8,128)(2,1)S(1)}, bf16[64,128,128]{2,1,0:T(8,128)(2,1)}, u32[]{:S(2)}) copy-start(bf16[64,128,128]{2,1,0:T(8,128)(2,1)} %get-tuple-element.99) | copy-start | bytes 6291460
  284.7 2.3 copy-start.2
  284.8 3.5 copy-start.3
Sparse Core Ops, SparseCore 0:
  24.8 84.2 all-reduce.11
  111.5 155.3 all-reduce.13
where the time goes:
time: 391 us; the launch traced here: 386 us
  local copies, waits for them, and re-layouts  144 us (37%)
  blocking collectives  65.6 us (17%)
  waiting for transfers between devices  59.4 us (15%)
  other arithmetic  43.6 us (11%)
  matrix products  28.3 us (7%)
  loops' own time  23.3 us (6%)
  between operations  21.6 us (6%)
    psum x2, waiting for transfers between devices, spread(): return lax.psum(kept, axis)  59.3 us
    unnamed x25, local copies, waits for them, and re-layouts  42.9 us
    unnamed x1, blocking collectives  40.6 us
    dot_general x2, matrix products, shards(): jnp.dot(a_masked, b_masked, preferred_element_type=jnp.float32)  27.9 us
    psum x2, blocking collectives, spread(): return lax.psum(kept, axis)  25 us
    another operation x1, loops' own time, prefix(): return lax.fori_loop(0, length, lap, start)  23.3 us
    gather x4, local copies, waits for them, and re-layouts, compact(): jnp.take(tiles, source, axis=0)  22.8 us
    dynamic_slice x32, local copies, waits for them, and re-layouts, lap(): new = combine(before, everything[k])  21.3 us
  transfers between devices with their start and end apart: 2, of which 1 were waited for; matrix products, arithmetic and copies ran while one was open for 22% of the time, Pallas kernels for 0%

commit v1 on v0

v1 whole, which is shorter than its diff:
```python
import functools

import jax
import jax.numpy as jnp
from jax import lax
from jax.experimental import pallas as pl
from jax.experimental.pallas import tpu as pltpu
from jax.sharding import PartitionSpec as P

TILE = 128
SECTIONS = 2
MOST = 64
CHUNKS = 16
MESH = pl.DeviceIdType.MESH
ANY = pl.BlockSpec(memory_space=pl.ANY)
SMEM = pl.BlockSpec(memory_space=pltpu.SMEM)
VMEM = pl.BlockSpec(memory_space=pltpu.VMEM)


def ring_place(index, n):
    half = n // 2
    turned = half + lax.rem(index - half + n // 4 + half, half)
    return jnp.where(index < half, index, turned)


def tile_at(ref, p, q):
    rows = pl.ds(pl.multiple_of(p * TILE, TILE), TILE)
    cols = pl.ds(pl.multiple_of(q * TILE, TILE), TILE)
    return ref.at[rows, cols]


def pack_kernel(tile_rows, panel, tile_cols, ratio, sections, a_flags, b_flags, a, b, a_out, b0_out, b1_out, sem):
    def gather(flags, src, out, rows, cols, first):
        def lap(i, rank):
            p, q = i // cols, lax.rem(i, cols)
            here = flags[first + p, q]

            @pl.when(here == 1)
            def _():
                pltpu.make_async_copy(tile_at(src, first + p, q), out.at[rank], sem).start()

            return rank + here

        return lax.fori_loop(0, rows * cols, lap, jnp.int32(0))

    total = jnp.int32(0)
    my_row, my_col = lax.axis_index("row"), lax.axis_index("col")
    mine_a = (sections[0] == my_col) | (sections[1] == my_col)
    total += lax.cond(mine_a, lambda: gather(a_flags, a, a_out, tile_rows, panel, 0), lambda: jnp.int32(0))
    for s, out in ((0, b0_out), (1, b1_out)):
        first = lax.rem(sections[s], ratio) * panel
        total += lax.cond(
            sections[s] // ratio == my_row,
            lambda: gather(b_flags, b, out, panel, tile_cols, first),
            lambda: jnp.int32(0),
        )

    @pl.loop(0, total)
    def _(i):
        pltpu.make_async_copy(tile_at(a, 0, 0), a_out.at[0], sem).wait()


def spread_kernel(root, owner, n_row, n_col, a_src, b_src, a_dst, b_dst, a_next, a_prev, a_recv, b_up, b_down, b_recv):
    my_row, my_col = lax.axis_index("row"), lax.axis_index("col")
    span = MOST // CHUNKS
    half = n_col // 2
    root_place = root if root < half else half + (root - half + n_col // 4) % half
    place = ring_place(my_col, n_col)
    dist = lax.rem(place - root_place + n_col, n_col)
    nxt = ring_place(lax.rem(place + 1, n_col), n_col)
    prv = ring_place(lax.rem(place + n_col - 1, n_col), n_col)
    a_root, b_root = dist == 0, my_row == owner
    to_next = dist < half
    to_prev = (dist == 0) | (dist > half + 1)
    to_up = (my_row >= owner) & (my_row < n_row - 1)
    to_down = (my_row <= owner) & (my_row > 0)
    up = jnp.minimum(my_row + 1, n_row - 1)
    down = jnp.maximum(my_row - 1, 0)

    barrier = pltpu.get_barrier_semaphore()

    def ready(when, row, col):
        @pl.when(when)
        def _():
            pl.semaphore_signal(barrier, inc=1, device_id=(row, col), device_id_type=MESH)

    ready((dist > 0) & (dist <= half), my_row, prv)
    ready(dist > half, my_row, nxt)
    ready(my_row > owner, down, my_col)
    ready(my_row < owner, up, my_col)
    targets = sum(when.astype(jnp.int32) for when in (to_next, to_prev, to_up, to_down))

    @pl.when(targets > 0)
    def _():
        pl.semaphore_wait(barrier, targets)

    def copy(src, dst, c, send, recv, row, col):
        part = pl.ds(c * span, span)
        return pltpu.make_async_remote_copy(
            src_ref=src.at[part],
            dst_ref=dst.at[part],
            send_sem=send.at[c],
            recv_sem=recv.at[c],
            device_id=(row, col),
            device_id_type=MESH,
        )

    def a_copies(src, c):
        return (
            (to_next, copy(src, a_dst, c, a_next, a_recv, my_row, nxt)),
            (to_prev, copy(src, a_dst, c, a_prev, a_recv, my_row, prv)),
        )

    def b_copies(src, c):
        return (
            (to_up, copy(src, b_dst, c, b_up, b_recv, up, my_col)),
            (to_down, copy(src, b_dst, c, b_down, b_recv, down, my_col)),
        )

    def start(copies):
        for when, one in copies:

            @pl.when(when)
            def _():
                one.start()

    @pl.when(b_root)
    def _():
        @pl.loop(0, CHUNKS)
        def _(c):
            start(b_copies(b_src, c))

    @pl.when(a_root)
    def _():
        @pl.loop(0, CHUNKS)
        def _(c):
            start(a_copies(a_src, c))

    def pass_a(c):
        @pl.when(jnp.logical_not(a_root))
        def _():
            copies = a_copies(a_dst, c)
            copies[0][1].wait_recv()
            start(copies)

    def pass_b(c):
        @pl.when(jnp.logical_not(b_root))
        def _():
            copies = b_copies(b_dst, c)
            copies[0][1].wait_recv()
            start(copies)

    lag = 2

    @pl.loop(0, CHUNKS)
    def _(c):
        pass_b(c)

        @pl.when((c >= lag) & (c < lag + CHUNKS // 2))
        def _():
            pass_a(2 * (c - lag))
            pass_a(2 * (c - lag) + 1)

    @pl.loop(0, CHUNKS)
    def _(c):
        for when, one in a_copies(a_dst, c) + b_copies(b_dst, c):

            @pl.when(when)
            def _():
                one.wait_send()


def spread(root, owner, n_row, n_col, a_src, b_src):
    return pl.pallas_call(
        functools.partial(spread_kernel, root, owner, n_row, n_col),
        out_shape=(
            jax.ShapeDtypeStruct(a_src.shape, a_src.dtype),
            jax.ShapeDtypeStruct(b_src.shape, b_src.dtype),
        ),
        in_specs=[ANY, ANY],
        out_specs=(ANY, ANY),
        scratch_shapes=[pltpu.SemaphoreType.DMA((CHUNKS,))] * 6,
        compiler_params=pltpu.CompilerParams(collective_id=root, has_side_effects=True),
        name=f"spread_{root}",
    )(a_src, b_src)


def product_kernel(
    tile_rows, panel, tile_cols, ratio, block, sections, a_flags, b_flags, slots, filled,
    a_mine, b0_mine, b1_mine, a0, a1, b0, b1, out, a_full, b_full, done, zero, sem, out_sem,
):
    my_row, my_col = lax.axis_index("row"), lax.axis_index("col")
    zero[...] = jnp.zeros_like(zero)
    slot_count = tile_rows * tile_cols

    def fill(flags, s, mine, got, is_mine, full, rows, cols, first_p, first_q):
        def lap(i, rank):
            p, q = i // cols, lax.rem(i, cols)
            here = flags[s, i]
            spot = tile_at(full, first_p + p, first_q + q)

            @pl.when((here == 1) & is_mine)
            def _():
                pltpu.make_async_copy(mine.at[rank], spot, sem).start()

            @pl.when((here == 1) & jnp.logical_not(is_mine))
            def _():
                pltpu.make_async_copy(got.at[rank], spot, sem).start()

            @pl.when(here == 0)
            def _():
                spot[...] = zero[...]

            return rank + here

        return lax.fori_loop(0, rows * cols, lap, jnp.int32(0))

    total = jnp.int32(0)
    for s, got_a, mine_b, got_b in ((0, a0, b0_mine, b0), (1, a1, b1_mine, b1)):
        total += fill(a_flags, s, a_mine, got_a, sections[s] == my_col, a_full, tile_rows, panel, 0, s * panel)
        total += fill(
            b_flags, s, mine_b, got_b, sections[s] // ratio == my_row, b_full, panel, tile_cols, s * panel, 0
        )

    @pl.loop(filled[0], slot_count)
    def _(k):
        pltpu.make_async_copy(zero, tile_at(out, k // tile_cols, lax.rem(k, tile_cols)), out_sem).start()

    @pl.loop(0, total)
    def _(i):
        pltpu.make_async_copy(a_mine.at[0], tile_at(a_full, 0, 0), sem).wait()

    across = tile_cols // block
    down = tile_rows // block

    @pl.loop(0, down * across)
    def _(step):
        i, j = step // across, lax.rem(step, across)
        rows = pl.ds(pl.multiple_of(i * block * TILE, block * TILE), block * TILE)
        cols = pl.ds(pl.multiple_of(j * block * TILE, block * TILE), block * TILE)
        done[rows, cols] = jnp.dot(
            a_full[rows, :], b_full[:, cols], preferred_element_type=jnp.float32
        ).astype(done.dtype)

    @pl.loop(0, slot_count)
    def _(i):
        slot = slots[i]

        @pl.when(slot >= 0)
        def _():
            pltpu.make_async_copy(
                tile_at(done, i // tile_cols, lax.rem(i, tile_cols)),
                tile_at(out, slot // tile_cols, lax.rem(slot, tile_cols)),
                out_sem,
            ).start()

    pltpu.make_async_copy(done, out, out_sem).wait()


def shards(n_row, n_col, a_matrix, a_flags, b_matrix, b_flags, sections):
    tile_rows, panel = a_flags.shape
    tile_cols = b_flags.shape[1]
    ratio = n_col // n_row
    dtype = a_matrix.dtype
    my_row, my_col = lax.axis_index("row"), lax.axis_index("col")

    tiles = jax.ShapeDtypeStruct((MOST, TILE, TILE), dtype)
    a_mine, b0_mine, b1_mine = pl.pallas_call(
        functools.partial(pack_kernel, tile_rows, panel, tile_cols, ratio),
        out_shape=(tiles, tiles, tiles),
        in_specs=[SMEM, SMEM, SMEM, ANY, ANY],
        out_specs=(VMEM, VMEM, VMEM),
        scratch_shapes=[pltpu.SemaphoreType.DMA],
        name="pack",
    )(sections, a_flags, b_flags, a_matrix, b_matrix)

    every = lax.all_gather(jnp.concatenate([a_flags, b_flags], axis=1), ("row", "col"))
    every = every.reshape(n_row, n_col, b_flags.shape[0], panel + tile_cols)

    got = []
    own_a, own_b = [], []
    common = jnp.zeros((n_row, n_col, tile_rows, tile_cols), jnp.float32)
    for s, b_mine in ((0, b0_mine), (1, b1_mine)):
        section = sections[s]
        branches = [
            functools.partial(spread, t, t // ratio, n_row, n_col) for t in range(n_col)
        ]
        got.append(lax.switch(section, branches, a_mine, b_mine))
        a_part = lax.dynamic_index_in_dim(every, section, 1, keepdims=False)[:, :, :panel]
        b_part = lax.dynamic_index_in_dim(every, section // ratio, 0, keepdims=False)
        b_part = lax.dynamic_slice_in_dim(b_part, section % ratio * panel, panel, 1)[:, :, panel:]
        own_a.append(lax.dynamic_index_in_dim(a_part, my_row, 0, keepdims=False).reshape(-1))
        own_b.append(lax.dynamic_index_in_dim(b_part, my_col, 0, keepdims=False).reshape(-1))
        common = common + jnp.einsum(
            "rpk,ckq->rcpq", a_part.astype(jnp.bfloat16), b_part.astype(jnp.bfloat16),
            preferred_element_type=jnp.float32,
        )
    occupied = (common > 0.5).astype(jnp.int32)
    counts = jnp.sum(occupied, axis=(2, 3)).reshape(-1)
    me = my_row * n_col + my_col
    offset = jnp.sum(jnp.where(jnp.arange(n_row * n_col) < me, counts, 0))
    own = occupied[my_row, my_col].reshape(-1)
    filled = jnp.sum(own)
    slots = jnp.where(own == 1, jnp.cumsum(own) - 1, -1).astype(jnp.int32)

    packed = pl.pallas_call(
        functools.partial(product_kernel, tile_rows, panel, tile_cols, ratio, 4),
        out_shape=jax.ShapeDtypeStruct((tile_rows * TILE, tile_cols * TILE), dtype),
        in_specs=[SMEM] * 5 + [ANY] * 7,
        out_specs=ANY,
        scratch_shapes=[
            pltpu.VMEM((tile_rows * TILE, SECTIONS * panel * TILE), dtype),
            pltpu.VMEM((SECTIONS * panel * TILE, tile_cols * TILE), dtype),
            pltpu.VMEM((tile_rows * TILE, tile_cols * TILE), dtype),
            pltpu.VMEM((TILE, TILE), dtype),
            pltpu.SemaphoreType.DMA,
            pltpu.SemaphoreType.DMA,
        ],
        compiler_params=pltpu.CompilerParams(vmem_limit_bytes=48 * 1024 * 1024),
        name="product",
    )(
        sections, jnp.stack(own_a), jnp.stack(own_b), slots, filled.reshape(1),
        a_mine, b0_mine, b1_mine, got[0][0], got[1][0], got[0][1], got[1][1],
    )
    slot_ids = jnp.arange(tile_rows * tile_cols, dtype=jnp.int32)
    places = jnp.where(slot_ids < filled, offset + slot_ids, -1).astype(jnp.int32)
    return packed, places.reshape(tile_rows, tile_cols)


def solution(mesh):
    return jax.shard_map(
        functools.partial(shards, mesh.shape["row"], mesh.shape["col"]),
        mesh=mesh,
        in_specs=(P("row", "col"), P("row", "col"), P("row", "col"), P("row", "col"), P()),
        out_specs=(P("row", "col"), P("row", "col")),
        check_vma=False,
    )
```

time: 391 us -> 226 us (0.58)
  the two profiles are of different devices: /device:TPU:0 before, /device:TPU:30 now
where the time goes in v1:
time: 226 us
  Pallas kernels  171 us (76%)
  blocking collectives  36.4 us (16%)
  between operations  9.87 us (4%)
  other arithmetic  5.19 us (2%)
  local copies, waits for them, and re-layouts  3.47 us (2%)
    pallas_call x2, Pallas kernels, spread(): pl.pallas_call(functools.partial(spread_kernel, root, owner, n_row, n_col...  124 us
    pallas_call x1, Pallas kernels, shards(): pl.pallas_call(functools.partial(product_kernel, tile_rows, panel, tile_c...  41.4 us
    all_gather x1, blocking collectives, shards(): lax.all_gather(jnp.concatenate([a_flags, b_flags], axis=1), ('row', 'col'))  36.4 us
    pallas_call x1, Pallas kernels, shards(): pl.pallas_call(functools.partial(pack_kernel, tile_rows, panel, tile_cols...  5.6 us

profile of v1, /device:TPU:30, one launch (start us, length us, event | category | flops | bytes accessed | tf_op | source)
XLA Modules:
  0.0 226.5 jit_solution(12389625872190264036)
XLA Ops:
  0.6 1.3 fusion.22
  11.1 0.8 copy.21.a_flags
  11.8 0.8 pad_add_fusion
  12.6 36.4 %all-gather = s32[512,24]{1,0:T(8,128)S(1)} all-gather(s32[16,24]{1,0:T(8,128)S(1)} %pad_add_fusion), channel_id=2, replica_groups=mesh['row'=4,'col'=8] {'row','col'}, dimensions={0}, use_global_device_ids=true | all-gather | bytes 50688 | tf_op jit(solution)/shard_map/all_gather | solution.py:277
  49.2 0.1 stack_reshape.12
  49.5 0.1 stack_reshape.15
  49.8 0.1 stack_reshape.13
  49.9 0.3 fusion.8
  50.2 0.3 fusion.4
  50.5 0.7 fusion.6
  51.2 0.7 fusion.17
  51.9 0.7 dynamic-slice_reduce_fusion
  52.6 0.1 copy.26
  52.7 0.1 eq.10
  52.8 1.9 add_select_fusion
  54.8 0.1 reshape.41
  54.8 0.3 reduce-window.9
  55.3 0.1 slice_reduce_fusion
  55.5 5.6 %pack.1 = (bf16[64,128,128]{2,1,0:T(8,128)(2,1)S(1)}, bf16[64,128,128]{2,1,0:T(8,128)(2,1)}, bf16[64,128,128]{2,1,0:T(8,128)(2,1)}) custom-call(s32[2]{0:T(128)} %sections.3, s32[16,8]{1,0:T(8,128)} %copy-done.1, s32[16,16]{1,0:T(8,128)} %b_flags.1, bf16[2048,1024]{1,0:T(8,128)(2,1)} %a.1, bf16[2048,2048]{1,0:T(8,128)(2,1)} %b.1), custom_call_target="tpu_custom_call" | custom-call | tf_op jit(solution)/shard_map/pack/pallas_call | solution.py:268
  61.1 46.0 %conditional.3 = ((bf16[64,128,128]{2,1,0:T(8,128)(2,1)}, bf16[64,128,128]{2,1,0:T(8,128)(2,1)})) conditional(s32[]{:T(128)} %clamp.23, (bf16[64,128,128]{2,1,0:T(8,128)(2,1)S(1)}, bf16[64,128,128]{2,1,0:T(8,128)(2,1)}) %tuple.57, (bf16[64,128,128]{2,1,0:T(8,128)(2,1)S(1)}, ...), branch_computations={%region_11.12_spmd, %region_12.13_spmd, %region_13.14_spmd, %regio... | conditional | bytes 8 | solution.py:288
  61.1 46.0 %spread_7.3 = (bf16[64,128,128]{2,1,0:T(8,128)(2,1)}, bf16[64,128,128]{2,1,0:T(8,128)(2,1)}) custom-call(bf16[64,128,128]{2,1,0:T(8,128)(2,1)S(1)} %get-tuple-element.94.a_src, bf16[64,128,128]{2,1,0:T(8,128)(2,1)} %get-tuple-element.95.b_src), custom_call_target="tpu_custom_call" | custom-call | tf_op jit(solution)/shard_map/cond/branch_7_fun/spread_7/pallas_call | solution.py:174
  107.1 78.0 %conditional.2 = ((bf16[64,128,128]{2,1,0:T(8,128)(2,1)}, bf16[64,128,128]{2,1,0:T(8,128)(2,1)})) conditional(s32[]{:T(128)} %clamp.22, (bf16[64,128,128]{2,1,0:T(8,128)(2,1)S(1)}, bf16[64,128,128]{2,1,0:T(8,128)(2,1)}) %tuple.56, (bf16[64,128,128]{2,1,0:T(8,128)(2,1)S(1)}, ...), branch_computations={%region_3.0_spmd, %region_4.0_spmd, %region_5.0_spmd, %region_6.0_... | conditional | bytes 8 | solution.py:288
  107.1 77.9 %spread_0.2 = (bf16[64,128,128]{2,1,0:T(8,128)(2,1)}, bf16[64,128,128]{2,1,0:T(8,128)(2,1)}) custom-call(bf16[64,128,128]{2,1,0:T(8,128)(2,1)S(1)} %get-tuple-element.64.a_src, bf16[64,128,128]{2,1,0:T(8,128)(2,1)} %get-tuple-element.65.b_src), custom_call_target="tpu_custom_call" | custom-call | tf_op jit(solution)/shard_map/cond/branch_0_fun/spread_0/pallas_call | solution.py:174
  185.1 41.4 %product.1 = bf16[2048,2048]{1,0:T(8,128)(2,1)} custom-call(s32[2]{0:T(128)S(1)} %copy-done, s32[2,128]{1,0:T(2,128)S(1)} %get-tuple-element.120.a_flags, s32[2,128]{1,0:T(2,128)S(1)} %get-tuple-element.121.b_flags, s32[256]{0:T(256)S(1)} %bitcast_select_fusion.1.slots, s32[1]{0:T(128)} %bitcast.15.filled, ...), custom_call_target="tpu_custom_call" | custom-call | tf_op jit(solution)/shard_map/product/pallas_call | solution.py:306
  (26 shorter events, 0.9 us)
Async XLA Ops:
  11.8 43.6 %copy-start.1 = (s32[16,8]{1,0:T(8,128)}, s32[16,8]{1,0:T(8,128)S(1)}, u32[]{:S(2)}) copy-start(s32[16,8]{1,0:T(8,128)S(1)} %copy.21.a_flags) | copy-start | bytes 1540
  107.1 78.0 %copy-start = (s32[2]{0:T(128)S(1)}, s32[2]{0:T(128)}, u32[]{:S(2)}) copy-start(s32[2]{0:T(128)} %sections.3) | copy-start | bytes 28

commit v2 on v1

--- a/solution.py
+++ b/solution.py
@@ -25,23 +25,24 @@
 
 def tile_at(ref, p, q):
     rows = pl.ds(pl.multiple_of(p * TILE, TILE), TILE)
-    cols = pl.ds(pl.multiple_of(q * TILE, TILE), TILE)
+    cols = pl.ds(q * TILE if isinstance(q, int) else pl.multiple_of(q * TILE, TILE), TILE)
     return ref.at[rows, cols]
 
 
 def pack_kernel(tile_rows, panel, tile_cols, ratio, sections, a_flags, b_flags, a, b, a_out, b0_out, b1_out, sem):
     def gather(flags, src, out, rows, cols, first):
-        def lap(i, rank):
-            p, q = i // cols, lax.rem(i, cols)
-            here = flags[first + p, q]
-
-            @pl.when(here == 1)
-            def _():
-                pltpu.make_async_copy(tile_at(src, first + p, q), out.at[rank], sem).start()
-
-            return rank + here
-
-        return lax.fori_loop(0, rows * cols, lap, jnp.int32(0))
+        def lap(p, rank):
+            for q in range(cols):
+                here = flags[first + p, q]
+
+                @pl.when(here == 1)
+                def _():
+                    pltpu.make_async_copy(tile_at(src, first + p, q), out.at[rank], sem).start()
+
+                rank = rank + here
+            return rank
+
+        return lax.fori_loop(0, rows, lap, jnp.int32(0))
 
     total = jnp.int32(0)
     my_row, my_col = lax.axis_index("row"), lax.axis_index("col")
@@ -60,7 +61,12 @@
         pltpu.make_async_copy(tile_at(a, 0, 0), a_out.at[0], sem).wait()
 
 
-def spread_kernel(root, owner, n_row, n_col, a_src, b_src, a_dst, b_dst, a_next, a_prev, a_recv, b_up, b_down, b_recv):
+def spread_kernel(root, owner, n_row, n_col, with_flags, *refs):
+    if with_flags:
+        a_src, b_src, flags, a_dst, b_dst, every, *sems = refs
+        a_next, a_prev, a_recv, b_up, b_down, b_recv, local, row_send, row_recv, col_send, col_recv = sems
+    else:
+        a_src, b_src, a_dst, b_dst, a_next, a_prev, a_recv, b_up, b_down, b_recv = refs
     my_row, my_col = lax.axis_index("row"), lax.axis_index("col")
     span = MOST // CHUNKS
     half = n_col // 2
@@ -84,15 +90,48 @@
         def _():
             pl.semaphore_signal(barrier, inc=1, device_id=(row, col), device_id_type=MESH)
 
-    ready((dist > 0) & (dist <= half), my_row, prv)
-    ready(dist > half, my_row, nxt)
-    ready(my_row > owner, down, my_col)
-    ready(my_row < owner, up, my_col)
-    targets = sum(when.astype(jnp.int32) for when in (to_next, to_prev, to_up, to_down))
-
-    @pl.when(targets > 0)
-    def _():
-        pl.semaphore_wait(barrier, targets)
+    if with_flags:
+        for k in range(1, n_row):
+            ready(True, lax.rem(my_row + k, n_row), my_col)
+        for k in range(1, n_col):
+            ready(True, my_row, lax.rem(my_col + k, n_col))
+        pl.semaphore_wait(barrier, n_row + n_col - 2)
+    else:
+        ready((dist > 0) & (dist <= half), my_row, prv)
+        ready(dist > half, my_row, nxt)
+        ready(my_row > owner, down, my_col)
+        ready(my_row < owner, up, my_col)
+        targets = sum(when.astype(jnp.int32) for when in (to_next, to_prev, to_up, to_down))
+
+        @pl.when(targets > 0)
+        def _():
+            pl.semaphore_wait(barrier, targets)
+
+    def along_row(k):
+        return pltpu.make_async_remote_copy(
+            src_ref=flags,
+            dst_ref=every.at[my_col, my_row],
+            send_sem=row_send.at[k],
+            recv_sem=row_recv.at[k],
+            device_id=(lax.rem(my_row + k, n_row), my_col),
+            device_id_type=MESH,
+        )
+
+    def along_col(k):
+        return pltpu.make_async_remote_copy(
+            src_ref=every.at[my_col],
+            dst_ref=every.at[my_col],
+            send_sem=col_send.at[k],
+            recv_sem=col_recv.at[k],
+            device_id=(my_row, lax.rem(my_col + k, n_col)),
+            device_id_type=MESH,
+        )
+
+    if with_flags:
+        own = pltpu.make_async_copy(flags, every.at[my_col, my_row], local)
+        own.start()
+        for k in range(1, n_row):
+            along_row(k).start()
 
     def copy(src, dst, c, send, recv, row, col):
         part = pl.ds(c * span, span)
@@ -150,6 +189,13 @@
             copies[0][1].wait_recv()
             start(copies)
 
+    if with_flags:
+        own.wait()
+        for k in range(1, n_row):
+            along_row(k).wait_recv()
+        for k in range(1, n_col):
+            along_col(k).start()
+
     lag = 2
 
     @pl.loop(0, CHUNKS)
@@ -169,20 +215,32 @@
             def _():
                 one.wait_send()
 
-
-def spread(root, owner, n_row, n_col, a_src, b_src):
+    if with_flags:
+        for k in range(1, n_row):
+            along_row(k).wait_send()
+        for k in range(1, n_col):
+            along_col(k).wait()
+
+
+def spread(root, owner, n_row, n_col, a_src, b_src, flags=None):
+    shapes = [jax.ShapeDtypeStruct(x.shape, x.dtype) for x in (a_src, b_src)]
+    operands = [a_src, b_src]
+    sems = [pltpu.SemaphoreType.DMA((CHUNKS,))] * 6
+    if flags is not None:
+        operands.append(flags)
+        shapes.append(jax.ShapeDtypeStruct((n_col, n_row) + flags.shape, flags.dtype))
+        sems += [pltpu.SemaphoreType.DMA] + [pltpu.SemaphoreType.DMA((n,)) for n in (n_row, n_row, n_col, n_col)]
     return pl.pallas_call(
-        functools.partial(spread_kernel, root, owner, n_row, n_col),
-        out_shape=(
-            jax.ShapeDtypeStruct(a_src.shape, a_src.dtype),
-            jax.ShapeDtypeStruct(b_src.shape, b_src.dtype),
+        functools.partial(spread_kernel, root, owner, n_row, n_col, flags is not None),
+        out_shape=tuple(shapes),
+        in_specs=[ANY] * len(operands),
+        out_specs=(ANY,) * len(shapes),
+        scratch_shapes=sems,
+        compiler_params=pltpu.CompilerParams(
+            collective_id=root + (n_col if flags is None else 0), has_side_effects=True
         ),
-        in_specs=[ANY, ANY],
-        out_specs=(ANY, ANY),
-        scratch_shapes=[pltpu.SemaphoreType.DMA((CHUNKS,))] * 6,
-        compiler_params=pltpu.CompilerParams(collective_id=root, has_side_effects=True),
-        name=f"spread_{root}",
-    )(a_src, b_src)
+        name=f"spread_{root}" if flags is None else f"spread_flags_{root}",
+    )(*operands)
 
 
 def product_kernel(
@@ -194,26 +252,26 @@
     slot_count = tile_rows * tile_cols
 
     def fill(flags, s, mine, got, is_mine, full, rows, cols, first_p, first_q):
-        def lap(i, rank):
-            p, q = i // cols, lax.rem(i, cols)
-            here = flags[s, i]
-            spot = tile_at(full, first_p + p, first_q + q)
-
-            @pl.when((here == 1) & is_mine)
-            def _():
-                pltpu.make_async_copy(mine.at[rank], spot, sem).start()
-
-            @pl.when((here == 1) & jnp.logical_not(is_mine))
-            def _():
-                pltpu.make_async_copy(got.at[rank], spot, sem).start()
-
-            @pl.when(here == 0)
-            def _():
-                spot[...] = zero[...]
-
-            return rank + here
-
-        return lax.fori_loop(0, rows * cols, lap, jnp.int32(0))
+        def run(src):
+            def lap(p, rank):
+                for q in range(cols):
+                    here = flags[s, p * cols + q]
+                    spot = tile_at(full, first_p + p, first_q + q)
+
+                    @pl.when(here == 1)
+                    def _():
+                        pltpu.make_async_copy(src.at[rank], spot, sem).start()
+
+                    @pl.when(here == 0)
+                    def _():
+                        spot[...] = jnp.zeros((TILE, TILE), full.dtype)
+
+                    rank = rank + here
+                return rank
+
+            return lax.fori_loop(0, rows, lap, jnp.int32(0))
+
+        return lax.cond(is_mine, lambda: run(mine), lambda: run(got))
 
     total = jnp.int32(0)
     for s, got_a, mine_b, got_b in ((0, a0, b0_mine, b0), (1, a1, b1_mine, b1)):
@@ -233,26 +291,30 @@
     across = tile_cols // block
     down = tile_rows // block
 
-    @pl.loop(0, down * across)
-    def _(step):
-        i, j = step // across, lax.rem(step, across)
+    @pl.loop(0, down)
+    def _(i):
         rows = pl.ds(pl.multiple_of(i * block * TILE, block * TILE), block * TILE)
-        cols = pl.ds(pl.multiple_of(j * block * TILE, block * TILE), block * TILE)
-        done[rows, cols] = jnp.dot(
-            a_full[rows, :], b_full[:, cols], preferred_element_type=jnp.float32
-        ).astype(done.dtype)
-
-    @pl.loop(0, slot_count)
-    def _(i):
-        slot = slots[i]
-
-        @pl.when(slot >= 0)
-        def _():
-            pltpu.make_async_copy(
-                tile_at(done, i // tile_cols, lax.rem(i, tile_cols)),
-                tile_at(out, slot // tile_cols, lax.rem(slot, tile_cols)),
-                out_sem,
-            ).start()
+
+        @pl.loop(0, across)
+        def _(j):
+            cols = pl.ds(pl.multiple_of(j * block * TILE, block * TILE), block * TILE)
+            done[rows, cols] = jnp.dot(
+                a_full[rows, :], b_full[:, cols], preferred_element_type=jnp.float32
+            ).astype(done.dtype)
+
+        @pl.loop(0, block)
+        def _(r):
+            p = i * block + r
+            for q in range(tile_cols):
+                slot = slots[p * tile_cols + q]
+
+                @pl.when(slot >= 0)
+                def _():
+                    pltpu.make_async_copy(
+                        tile_at(done, p, q),
+                        tile_at(out, lax.div(slot, tile_cols), lax.rem(slot, tile_cols)),
+                        out_sem,
+                    ).start()
 
     pltpu.make_async_copy(done, out, out_sem).wait()
 
@@ -274,21 +336,22 @@
         name="pack",
     )(sections, a_flags, b_flags, a_matrix, b_matrix)
 
-    every = lax.all_gather(jnp.concatenate([a_flags, b_flags], axis=1), ("row", "col"))
-    every = every.reshape(n_row, n_col, b_flags.shape[0], panel + tile_cols)
-
+    flags = jnp.concatenate([a_flags, b_flags], axis=1)
+    flags = jnp.pad(flags, ((0, 0), (0, -flags.shape[1] % TILE)))
     got = []
+    for s, b_mine in ((0, b0_mine), (1, b1_mine)):
+        operands = (a_mine, b_mine) if s else (a_mine, b_mine, flags)
+        branches = [functools.partial(spread, t, t // ratio, n_row, n_col) for t in range(n_col)]
+        got.append(lax.switch(sections[s], branches, *operands))
+    every = got[0][2]
+
     own_a, own_b = [], []
     common = jnp.zeros((n_row, n_col, tile_rows, tile_cols), jnp.float32)
-    for s, b_mine in ((0, b0_mine), (1, b1_mine)):
+    for s in range(SECTIONS):
         section = sections[s]
-        branches = [
-            functools.partial(spread, t, t // ratio, n_row, n_col) for t in range(n_col)
-        ]
-        got.append(lax.switch(section, branches, a_mine, b_mine))
-        a_part = lax.dynamic_index_in_dim(every, section, 1, keepdims=False)[:, :, :panel]
-        b_part = lax.dynamic_index_in_dim(every, section // ratio, 0, keepdims=False)
-        b_part = lax.dynamic_slice_in_dim(b_part, section % ratio * panel, panel, 1)[:, :, panel:]
+        a_part = lax.dynamic_index_in_dim(every, section, 0, keepdims=False)[:, :, :panel]
+        b_part = lax.dynamic_index_in_dim(every, section // ratio, 1, keepdims=False)
+        b_part = lax.dynamic_slice_in_dim(b_part, section % ratio * panel, panel, 1)[:, :, panel : panel + tile_cols]
         own_a.append(lax.dynamic_index_in_dim(a_part, my_row, 0, keepdims=False).reshape(-1))
         own_b.append(lax.dynamic_index_in_dim(b_part, my_col, 0, keepdims=False).reshape(-1))
         common = common + jnp.einsum(

time: 226 us -> 184 us (0.81)
  the two profiles are of different devices: /device:TPU:30 before, /device:TPU:0 now
where the time goes in v2:
time: 184 us; the launch traced here: 182 us
  Pallas kernels  163 us (89%)
  between operations  9.9 us (5%)
  other arithmetic  5.07 us (3%)
  local copies, waits for them, and re-layouts  3.58 us (2%)
    pallas_call x2, Pallas kernels, spread(): pl.pallas_call(functools.partial(spread_kernel, root, owner, n_row, n_col...  129 us
    pallas_call x1, Pallas kernels, shards(): pl.pallas_call(functools.partial(product_kernel, tile_rows, panel, tile_c...  30.8 us

profile of v2, /device:TPU:0, one launch (start us, length us, event | category | flops | bytes accessed | tf_op | source)
XLA Modules:
  0.0 182.1 jit_solution(543405050171928666)
XLA Ops:
  0.6 1.3 fusion.22
  11.1 0.8 copy.21.a_flags
  11.8 0.8 pad_add_fusion
  12.6 2.9 %pack.1 = (bf16[64,128,128]{2,1,0:T(8,128)(2,1)S(1)}, bf16[64,128,128]{2,1,0:T(8,128)(2,1)}, bf16[64,128,128]{2,1,0:T(8,128)(2,1)}) custom-call(s32[2]{0:T(128)} %sections.3, s32[16,8]{1,0:T(8,128)} %copy-done.1, s32[16,16]{1,0:T(8,128)} %b_flags.1, bf16[2048,1024]{1,0:T(8,128)(2,1)} %a.1, bf16[2048,2048]{1,0:T(8,128)(2,1)} %b.1), custom_call_target="tpu_custom_call" | custom-call | tf_op jit(solution)/shard_map/pack/pallas_call | solution.py:330
  15.6 52.1 %conditional.3 = ((bf16[64,128,128]{2,1,0:T(8,128)(2,1)}, bf16[64,128,128]{2,1,0:T(8,128)(2,1)})) conditional(s32[]{:T(128)} %clamp.23, (bf16[64,128,128]{2,1,0:T(8,128)(2,1)S(1)}, bf16[64,128,128]{2,1,0:T(8,128)(2,1)}) %tuple.57, (bf16[64,128,128]{2,1,0:T(8,128)(2,1)S(1)}, ...), branch_computations={%region_11.12_spmd, %region_12.13_spmd, %region_13.14_spmd, %regio... | conditional | bytes 8 | solution.py:345
  15.6 52.0 %spread_2.1 = (bf16[64,128,128]{2,1,0:T(8,128)(2,1)}, bf16[64,128,128]{2,1,0:T(8,128)(2,1)}) custom-call(bf16[64,128,128]{2,1,0:T(8,128)(2,1)S(1)} %get-tuple-element.108.refs_0_, bf16[64,128,128]{2,1,0:T(8,128)(2,1)} %get-tuple-element.109.refs_1_), custom_call_target="tpu_custom_call" | custom-call | tf_op jit(solution)/shard_map/cond/branch_2_fun/spread_2/pallas_call | solution.py:233
  67.6 77.1 %conditional.2 = ((bf16[64,128,128]{2,1,0:T(8,128)(2,1)}, bf16[64,128,128]{2,1,0:T(8,128)(2,1)}, s32[8,4,16,128]{3,2,1,0:T(8,128)S(1)})) conditional(s32[]{:T(128)} %clamp.22, (bf16[64,128,128]{2,1,0:T(8,128)(2,1)S(1)}, bf16[64,128,128]{2,1,0:T(8,128)(2,1)}, s32[16,128]{1,0:T(8,128)S(1)}) %tuple.56, ...), branch_computations={%region_0.1_spmd, %region_1.2_spmd, %region_2.3_spmd, %region_3.4_... | conditional | bytes 8 | solution.py:345
  67.7 77.1 %spread_flags_6.1 = (bf16[64,128,128]{2,1,0:T(8,128)(2,1)}, bf16[64,128,128]{2,1,0:T(8,128)(2,1)}, s32[8,4,16,128]{3,2,1,0:T(8,128)S(1)}) custom-call(bf16[64,128,128]{2,1,0:T(8,128)(2,1)S(1)} %get-tuple-element.98.refs_0_, bf16[64,128,128]{2,1,0:T(8,128)(2,1)} %get-tuple-element.99.refs_1_, s32[16,128]{1,0:T(8,128)S(1)} %get-tuple-element.100.refs_2_), custom_call_target="tpu_custom_call" | custom-call | tf_op jit(solution)/shard_map/cond/branch_6_fun/spread_flags_6/pallas_call | solution.py:233
  145.0 0.1 stack_reshape.15
  145.1 0.1 copy.23
  145.3 0.3 fusion.8
  145.7 0.1 stack_reshape.12
  145.7 0.1 copy.25
  145.9 0.3 fusion.4
  146.3 0.1 stack_reshape.13
  146.4 0.7 fusion.6
  147.1 0.6 fusion.17
  147.8 0.7 dynamic-slice_reduce_fusion
  148.4 0.1 copy.27
  148.5 0.1 eq.10
  148.6 1.9 %add_select_fusion = s32[16,16]{1,0:T(8,128)} fusion(s32[]{:T(128)} %fusion.17, s32[]{:T(128)} %dynamic-slice_reduce_fusion), kind=kLoop, calls=%fused_computation.19 | loop fusion | flops 1280 | bytes 1032 | tf_op jit(solution)/shard_map/jit(_where)/select_n | solution.py:389
  150.6 0.3 reduce-window.9
  151.0 0.1 slice_reduce_fusion
  151.2 30.8 %product.1 = bf16[2048,2048]{1,0:T(8,128)(2,1)} custom-call(s32[2]{0:T(128)S(1)} %copy-done, s32[2,128]{1,0:T(2,128)S(1)} %get-tuple-element.146.a_flags, s32[2,128]{1,0:T(2,128)S(1)} %get-tuple-element.147.b_flags, s32[256]{0:T(256)S(1)} %bitcast_select_fusion.1.slots, s32[1]{0:T(128)} %bitcast.14.filled, ...), custom_call_target="tpu_custom_call" | custom-call | tf_op jit(solution)/shard_map/product/pallas_call | solution.py:369
  (26 shorter events, 0.8 us)
Async XLA Ops:
  11.8 0.8 copy-start.1
  144.7 6.5 %copy-start = (s32[2]{0:T(128)S(1)}, s32[2]{0:T(128)}, u32[]{:S(2)}) copy-start(s32[2]{0:T(128)} %sections.3) | copy-start | bytes 28
